TPU v7x, 256 devices: a whole 4x4x8 slice. The times are simulated.
256 devices in a mesh: task: 8 (over z), shard: 8 (over y, core), rep: 4 (over x).
Axes of the slice: x: 4, y: 4, z: 8, core: 2. Of those that a mesh axis runs over, the one named last changes fastest.
Arguments:
- deltas: bfloat16 [16, 256, 16, 8192], P('task', None, None, ('shard', 'rep')), may hold values from -4 to 4
- base: bfloat16 [256, 16, 8, 1024], P(('task', 'shard'), None, None, 'rep'), may hold values from -60 to 60
- sel_index: int32 [16, 64], replicated, may hold values from 0 to 255, as said below
- sel_count: int32 [16], replicated, may hold values from 1 to 64
- scale_num: int32 [16], replicated, may hold values from 1 to 12
Outputs:
- merged: bfloat16 [256, 16, 8192], P(('task', 'shard'))
Inputs may be any that keep to these rules, and one draw needn't show every extreme that they name: `sel_index`: for task i the first sel_count[i] entries are distinct and ascending; at most 1 of them lie in any aligned group of 4 blocks, and in every draw some group holds 1 selected blocks of every task, and some task selects 1 block in every group. Later entries are block numbers that are not selected.
All inputs are finite; a program needn't handle non-finite values.
Results may differ from a plain program's by a relative error of at most 0.00045.
Values may be sent and summed in bfloat16 or wider, within the bound.
No kernel may reach another device: no remote copies, remote signals or barrier semaphores. Data moves between devices by JAX's collectives and lax.ppermute only.
A program may use at most 64 MiB of HBM per device.

v0:
```python
import functools

import jax
import jax.numpy as jnp
from jax import lax
from jax.sharding import Mesh
from jax.sharding import PartitionSpec as P

LAYERS = 4
SHARD = ("shard_0", "shard_1")
TASK_SHARD = ("task", "shard_0", "shard_1")
TASK_SHARD_REP = ("task", "shard_0", "shard_1", "rep")
SHARD_REP = ("shard_0", "shard_1", "rep")


denominator = 8.0
epsilon = 1e-06


def over_axes(shard, axes):
    return functools.reduce(lax.psum, axes, shard)


def joined_along(blocks, dim):
    blocks = jnp.moveaxis(blocks, 0, dim)
    shape = blocks.shape
    return blocks.reshape(*shape[:dim], shape[dim] * shape[dim + 1], *shape[dim + 2 :])


def sent_to_all(shard, axis):
    copies = jnp.broadcast_to(shard, (lax.axis_size(axis), *shard.shape))
    return lax.all_to_all(copies, axis, split_axis=0, concat_axis=0, tiled=True)


def gather_directly(shard, axis, dim):
    return joined_along(sent_to_all(shard, axis), dim)


def slot_tables(sel_index, sel_count, own_blocks, owners):
    entries = jnp.arange(sel_index.shape[1], dtype=jnp.int32)
    valid = entries[None, :] < sel_count[:, None]
    owner_of = sel_index // own_blocks
    owner_ids = jnp.arange(owners, dtype=jnp.int32)
    earlier = valid[:, :, None] & (owner_of[:, :, None] < owner_ids[None, None, :])
    within = valid[:, :, None] & (owner_of[:, :, None] == owner_ids[None, None, :])
    before = jnp.sum(earlier.astype(jnp.int32), axis=1)
    inside = jnp.sum(within.astype(jnp.int32), axis=1)
    return (before, inside)


def slot_blocks(sel_index, start, capacity):
    limit = sel_index.shape[1] - 1
    where_at = jnp.minimum(
        start[:, :, None] + jnp.arange(capacity, dtype=jnp.int32)[None, None, :], limit
    )
    flat = jnp.take_along_axis(sel_index, where_at.reshape(sel_index.shape[0], -1), axis=1)
    return flat.reshape(where_at.shape)


def layer_sums(values, onehot):
    per_block = jnp.sum(values * values, axis=(1, 2, 3))
    return jnp.sum(per_block[:, None] * onehot, axis=0)


def shards(deltas, base, sel_index, sel_count, scale_num):
    task_dev = deltas.shape[0]
    nb_all = deltas.shape[1]
    rows = deltas.shape[2]
    width = deltas.shape[3]
    n_task = lax.axis_size("task")
    n_shard = lax.axis_size(SHARD)
    owners = n_task * n_shard
    own_blocks = base.shape[0]
    capacity = own_blocks // 4
    my_task = lax.axis_index("task")
    owner_me = my_task * n_shard + lax.axis_index(SHARD)
    before, inside = slot_tables(sel_index, sel_count, own_blocks, owners)
    base_wide = base.astype(jnp.float32)
    layer_span = nb_all // LAYERS
    layer_of = (owner_me * own_blocks + jnp.arange(own_blocks, dtype=jnp.int32)) // layer_span
    onehot = (layer_of[:, None] == jnp.arange(LAYERS, dtype=jnp.int32)[None, :]).astype(jnp.float32)
    base_sq = layer_sums(base_wide, onehot)
    first = my_task * task_dev
    mine_index = lax.dynamic_slice_in_dim(sel_index, first, task_dev, 0)
    mine_before = lax.dynamic_slice_in_dim(before, first, task_dev, 0)
    mine_inside = lax.dynamic_slice_in_dim(inside, first, task_dev, 0)
    chosen = jnp.transpose(slot_blocks(mine_index, mine_before, capacity), (1, 0, 2))
    live = jnp.transpose(
        jnp.arange(capacity, dtype=jnp.int32)[None, None, :] < mine_inside[:, :, None], (1, 0, 2)
    )
    holder = jnp.broadcast_to(jnp.arange(task_dev, dtype=jnp.int32)[None, :, None], chosen.shape)
    outgoing = deltas[holder, chosen]
    outgoing = jnp.where(live[:, :, :, None, None], outgoing, jnp.zeros((), jnp.bfloat16))
    outgoing = outgoing.reshape(n_task, n_shard, task_dev, capacity, rows, width)
    flat_out = outgoing.reshape(owners, task_dev, capacity, rows, width)
    incoming = lax.all_to_all(flat_out, TASK_SHARD, split_axis=0, concat_axis=0, tiled=True)
    incoming = incoming.reshape(n_task, n_shard, task_dev, capacity, rows, width)
    start_me = lax.dynamic_slice_in_dim(before, owner_me, 1, 1)
    count_me = lax.dynamic_slice_in_dim(inside, owner_me, 1, 1)
    arrived = slot_blocks(sel_index, start_me, capacity)[:, 0, :]
    arrived_live = jnp.arange(capacity, dtype=jnp.int32)[None, :] < count_me
    local_block = arrived - owner_me * own_blocks
    factor = scale_num.astype(jnp.float32) / denominator
    match = (
        local_block[None, :, :] == jnp.arange(own_blocks, dtype=jnp.int32)[:, None, None]
    ) & arrived_live[None, :, :]
    weight = jnp.where(match, factor[None, :, None], 0.0)
    weight = weight.reshape(own_blocks, n_task, task_dev, capacity).astype(jnp.bfloat16)
    combined = jnp.einsum("jtak,tsakrc->jrsc", weight, incoming, preferred_element_type=jnp.float32)
    merged_raw = base_wide + combined
    merged_sq = layer_sums(merged_raw, onehot)
    base_total, merged_total = (
        over_axes(base_sq, TASK_SHARD_REP),
        over_axes(merged_sq, TASK_SHARD_REP),
    )
    ratio = jnp.sqrt((base_total + epsilon) / (merged_total + epsilon))
    block_ratio = jnp.sum(onehot * ratio[None, :], axis=1)
    result = (merged_raw * block_ratio[:, None, None, None]).astype(jnp.bfloat16)
    copies = gather_directly(result, "rep", 3)
    return copies.reshape(own_blocks, rows, -1)


def solution(mesh):
    torus = Mesh(
        mesh.devices.reshape(mesh.shape["task"], 4, 2, mesh.shape["rep"]),
        ("task", "shard_0", "shard_1", "rep"),
    )
    placed = (P("task", None, None, SHARD_REP), P(TASK_SHARD, None, None, "rep"), P(), P(), P())
    return jax.shard_map(
        shards, mesh=torus, in_specs=placed, out_specs=P(TASK_SHARD, None, None), check_vma=False
    )
```

profile of v0, /device:TPU:1, one launch (start us, length us, event | category | flops | bytes accessed | tf_op | source)
XLA Modules:
  0.0 107.2 jit_solution(14761251280044841469)
XLA Ops:
  0.0 0.0 copy-start
  0.0 0.0 copy-start.2
  0.0 0.8 add_select_fusion
  0.8 0.7 constant_dynamic-slice_fusion
  1.5 0.7 iota_compare_fusion.2
  2.2 0.4 convert_reduce_fusion.1
  2.6 0.1 reshape.192
  2.7 1.5 %gather_fusion.1 = s32[128]{0:T(128)S(1)} fusion(s32[2,64]{1,0:T(2,128)S(1)} %constant_dynamic-slice_fusion, s32[128]{0:T(128)S(1)} %reshape.192), kind=kCustom, calls=%fused_computation.1 | custom fusion | bytes 2048 | tf_op jit(solution)/shard_map/jit(take_along_axis)/gather | solution.py:56
  4.2 0.1 reshape.195
  4.4 0.1 copy.62
  4.5 0.1 copy.63
  4.6 0.1 reshape.186
  4.7 0.0 copy-start.1
  4.7 3.1 %gather_fusion = bf16[128,16,256]{2,1,0:T(8,128)(2,1)S(1)} fusion(bf16[2,256,16,256]{3,2,1,0:T(8,128)(2,1)} %param.5, s32[128]{0:T(128)S(1)} %reshape.186), kind=kCustom, calls=%fused_computation | custom fusion | bytes 2098176 | tf_op jit(solution)/shard_map/gather | solution.py:92
  7.8 1.2 %broadcast_select_fusion = bf16[64,2,1,16,256]{4,3,1,2,0:T(8,128)(2,1)} fusion(bf16[64,2,1,16,256]{4,3,1,2,0:T(8,128)(2,1)S(1)} %bitcast.44, pred[64,2]{1,0:T(8,128)(4,1)S(1)} %copy.62), kind=kLoop, calls=%fused_computation.5 | loop fusion | flops 524288 | bytes 2097280 | tf_op jit(solution)/shard_map/jit(_where)/select_n | solution.py:93
  9.0 13.1 %all-to-all-start = ((bf16[64,2,1,16,256]{4,3,1,2,0:T(8,128)(2,1)}), bf16[64,2,1,16,256]{4,3,1,2,0:T(8,128)(2,1)S(1)}, u32[]{:S(2)}, u32[]{:S(2)}) async-start(bf16[64,2,1,16,256]{4,3,1,2,0:T(8,128)(2,1)} %broadcast_select_fusion), calls=%async_computation | async-start | bytes 2097152 | tf_op jit(solution)/shard_map/all_to_all | solution.py:96
  22.2 0.0 copy-done.2
  22.2 0.1 broadcast_in_dim.44
  22.3 0.1 copy.69
  22.4 0.2 fusion.6
  22.6 0.1 and.71
  22.6 0.1 copy.68
  22.7 0.2 fusion.7
  23.0 0.1 copy.75
  23.1 0.1 copy.76
  23.1 0.1 or_reduce_fusion
  23.3 0.0 copy-done
  23.3 0.7 gather_fusion.2
  23.9 0.1 copy.66
  24.0 0.2 subtract_reduce_fusion
  24.2 0.1 eq.52
  24.3 0.1 copy.67
  24.4 25.9 %all-to-all-done = bf16[64,2,1,16,256]{4,3,1,2,0:T(8,128)(2,1)S(1)} async-done(((bf16[64,2,1,16,256]{4,3,1,2,0:T(8,128)(2,1)}), bf16[64,2,1,16,256]{4,3,1,2,0:T(8,128)(2,1)S(1)}, u32[]{:S(2)}, u32[]{:S(2)}) %all-to-all-start) | async-done | bytes 1048608 | tf_op jit(solution)/shard_map/all_to_all | solution.py:96
  50.3 0.7 convolution_bitcast_fusion
  51.0 0.0 copy-done.1
  51.0 0.4 fusion.1
  51.4 0.1 select_reduce_fusion.2
  51.5 12.4 %all-reduce = (f32[4]{0:T(128)S(1)}, f32[4]{0:T(128)S(1)}) all-reduce(f32[4]{0:T(128)S(1)} %get-tuple-element.10, f32[4]{0:T(128)S(1)} %get-tuple-element.9), channel_id=1, replica_groups=mesh['task'=8,'shard_0'=4,'shard_1'=2,'rep'=4] {'task'}, use_global_device_ids=true, to_apply=%region_10.11 | all-reduce | flops 8 | bytes 64 | tf_op jit(solution)/shard_map/psum | solution.py:21
  63.9 7.5 %all-reduce.2 = (f32[4]{0:T(128)S(1)}, f32[4]{0:T(128)S(1)}) all-reduce(f32[4]{0:T(128)S(1)} %get-tuple-element.11, f32[4]{0:T(128)S(1)} %get-tuple-element.12), channel_id=1, replica_groups=mesh['task'=8,'shard_0'=4,'shard_1'=2,'rep'=4] {'shard_0'}, use_global_device_ids=true, to_apply=%region_11.12 | all-reduce | flops 8 | bytes 64 | tf_op jit(solution)/shard_map/psum | solution.py:21
  71.5 8.5 %all-reduce.3 = (f32[4]{0:T(128)S(1)}, f32[4]{0:T(128)S(1)}) all-reduce(f32[4]{0:T(128)S(1)} %get-tuple-element.15, f32[4]{0:T(128)S(1)} %get-tuple-element.16), channel_id=1, replica_groups=mesh['task'=8,'shard_0'=4,'shard_1'=2,'rep'=4] {'shard_1'}, use_global_device_ids=true, to_apply=%region_12.13 | all-reduce | flops 8 | bytes 64 | tf_op jit(solution)/shard_map/psum | solution.py:21
  80.0 8.4 %all-reduce.1 = (f32[4]{0:T(128)S(1)}, f32[4]{0:T(128)S(1)}) all-reduce(f32[4]{0:T(128)S(1)} %get-tuple-element.17, f32[4]{0:T(128)S(1)} %get-tuple-element.18), channel_id=1, replica_groups=mesh['task'=8,'shard_0'=4,'shard_1'=2,'rep'=4] {'rep'}, use_global_device_ids=true, to_apply=%region_13.14 | all-reduce | flops 8 | bytes 64 | tf_op jit(solution)/shard_map/psum | solution.py:21
  88.4 0.2 select_reduce_fusion
  88.6 0.3 multiply_convert_fusion
  88.9 0.1 broadcast_in_dim.76
  89.0 15.3 %all_to_all.10 = bf16[4,4,16,8,256]{4,3,2,1,0:T(8,128)(2,1)S(1)} all-to-all(bf16[4,4,16,8,256]{4,3,2,1,0:T(8,128)(2,1)S(1)} %broadcast_in_dim.76), channel_id=1, replica_groups=mesh['task'=8,'shard_0'=4,'shard_1'=2,'rep'=4] {'rep'}, dimensions={0} | all-to-all | bytes 2097152 | tf_op jit(solution)/shard_map/all_to_all | solution.py:32
  104.3 1.4 %copy.72 = bf16[4,16,8,4,256]{4,3,2,1,0:T(4,128)(2,1)S(1)} copy(bf16[4,16,8,4,256]{4,2,1,0,3:T(8,128)(2,1)S(1)} %bitcast.45) | data formatting | bytes 2097152 | tf_op jit(solution)/shard_map/transpose | solution.py:25
  105.7 1.6 %reshape_reshape.3 = bf16[4,16,8192]{2,1,0:T(8,128)(2,1)} reshape(bf16[4,16,8,4,256]{4,3,2,1,0:T(4,128)(2,1)S(1)} %copy.72) | data formatting | bytes 2097152 | tf_op jit(solution)/shard_map/reshape;reshape | solution.py:120
  (12 shorter events, 0.1 us)
Async XLA Ops:
  0.0 23.3 %copy-start = (s32[16,64]{1,0:T(8,128)S(1)}, s32[16,64]{1,0:T(8,128)}, u32[]{:S(2)}) copy-start(s32[16,64]{1,0:T(8,128)} %param.7) | copy-start | bytes 12292
  0.0 22.2 %copy-start.2 = (s32[16]{0:T(128)S(1)}, s32[16]{0:T(128)}, u32[]{:S(2)}) copy-start(s32[16]{0:T(128)} %param.9) | copy-start | bytes 196
  4.7 46.3 %copy-start.1 = (bf16[4,16,8,256]{3,2,1,0:T(8,128)(2,1)S(1)}, bf16[4,16,8,256]{3,2,1,0:T(8,128)(2,1)}, u32[]{:S(2)}) copy-start(bf16[4,16,8,256]{3,2,1,0:T(8,128)(2,1)} %param.6) | copy-start | bytes 786436
  9.0 41.3 %all-to-all-start = ((bf16[64,2,1,16,256]{4,3,1,2,0:T(8,128)(2,1)}), bf16[64,2,1,16,256]{4,3,1,2,0:T(8,128)(2,1)S(1)}, u32[]{:S(2)}, u32[]{:S(2)}) async-start(bf16[64,2,1,16,256]{4,3,1,2,0:T(8,128)(2,1)} %broadcast_select_fusion), calls=%async_computation | async-start | bytes 2097152 | tf_op jit(solution)/shard_map/all_to_all | solution.py:96
where the time goes:
time: 109 us; the launch traced here: 107 us
  blocking collectives  52.1 us (48%)
  waiting for transfers between devices  25.9 us (24%)
  starting transfers between devices  13.1 us (12%)
  local copies, waits for them, and re-layouts  10.3 us (9%)
  other arithmetic  4.84 us (4%)
    psum x4, blocking collectives, over_axes(): return functools.reduce(lax.psum, axes, shard)  36.9 us
    all_to_all x1, waiting for transfers between devices, shards(): lax.all_to_all(flat_out, TASK_SHARD, split_axis=0, concat_axis=0, tiled=T...  25.9 us
    all_to_all x1, blocking collectives, sent_to_all(): return lax.all_to_all(copies, axis, split_axis=0, concat_axis=0, tiled=True)  15.3 us
    all_to_all x1, starting transfers between devices, shards(): lax.all_to_all(flat_out, TASK_SHARD, split_axis=0, concat_axis=0, tiled=T...  13.1 us
    gather x1, local copies, waits for them, and re-layouts, shards(): outgoing = deltas[holder, chosen]  3.09 us
    gather x6, local copies, waits for them, and re-layouts, slot_blocks(): jnp.take_along_axis(sel_index, where_at.reshape(sel_index.shape[0], -1),...  2.43 us
  transfers between devices with their start and end apart: 1, of which 1 were waited for; matrix products, arithmetic and copies ran while one was open for 2% of the time, Pallas kernels for 0%

commit v1 on v0

v1 whole, which is shorter than its diff:
```python
import functools

import jax
import jax.numpy as jnp
from jax import lax
from jax.experimental import pallas as pl
from jax.experimental.pallas import tpu as pltpu
from jax.sharding import Mesh
from jax.sharding import PartitionSpec as P

TASK = ("layer", "half")
SHARD = ("shard_0", "shard_1")
OWNER = ("layer", "half", "shard_0", "shard_1")
SAME_LAYER = ("half", "shard_0", "shard_1", "rep")
LAYERS = 4
DENOMINATOR = 8.0
EPSILON = 1e-06
LANES = 128


KERNEL = pltpu.CompilerParams(vmem_limit_bytes=16 * 2**20)


def cost(flops, bytes_accessed):
    return pl.CostEstimate(flops=flops, bytes_accessed=bytes_accessed, transcendentals=0)


def pick_kernel(own, sel_ref, count_ref, deltas_ref, out_ref, table, sem):
    owners, task_dev = out_ref.shape[:2]
    first = lax.axis_index(TASK) * task_dev
    entries = sel_ref.shape[1]

    def start_row(o, carry):
        for a in range(task_dev):
            table[a, o] = o * own
        return carry

    lax.fori_loop(0, owners, start_row, 0, unroll=8)

    for a in range(task_dev):
        count = count_ref[first + a]

        def note(k, carry, a=a):
            block = sel_ref[first + a, k]
            table[a, block // own] = block
            return carry

        lax.fori_loop(0, count, note, 0)

    def copy_row(o, carry):
        for a in range(task_dev):
            pltpu.make_async_copy(deltas_ref.at[a, table[a, o]], out_ref.at[o, a], sem).start()
        return carry

    lax.fori_loop(0, owners, copy_row, 0, unroll=4)
    pltpu.make_async_copy(out_ref, out_ref, sem).wait()


def pick(sel_index, sel_count, deltas, owners, own):
    task_dev, _, rows, width = deltas.shape
    smem = pl.BlockSpec(memory_space=pltpu.SMEM)
    return pl.pallas_call(
        functools.partial(pick_kernel, own),
        out_shape=jax.ShapeDtypeStruct((owners, task_dev, rows, width), deltas.dtype),
        in_specs=[smem, smem, pl.BlockSpec(memory_space=pl.ANY)],
        out_specs=pl.BlockSpec(memory_space=pltpu.VMEM),
        scratch_shapes=[pltpu.SMEM((task_dev, owners), jnp.int32), pltpu.SemaphoreType.DMA],
        cost_estimate=cost(10_000_000, 2 * owners * task_dev * rows * width * 2),
        name="pick",
    )(sel_index, sel_count, deltas)


def combine_kernel(incoming_ref, base_ref, weight_ref, merged_ref, sums_ref):
    n_task, groups, task_dev, rows, width = incoming_ref.shape
    own = base_ref.shape[0]

    def group(s, sums):
        base_sum, merged_sum = sums
        total = [base_ref[j, s].astype(jnp.float32) for j in range(own)]
        for j in range(own):
            base_sum = base_sum + jnp.sum(total[j] * total[j], axis=0, keepdims=True)
        for t in range(n_task):
            for a in range(task_dev):
                delta = incoming_ref[t, s, a].astype(jnp.float32)
                for j in range(own):
                    total[j] = total[j] + weight_ref[j, t * task_dev + a : t * task_dev + a + 1] * delta
        for j in range(own):
            merged_ref[j, s] = total[j]
            merged_sum = merged_sum + jnp.sum(total[j] * total[j], axis=0, keepdims=True)
        return base_sum, merged_sum

    zero = jnp.zeros((1, width), jnp.float32)
    base_sum, merged_sum = lax.fori_loop(0, groups, group, (zero, zero))
    fold = lambda row: functools.reduce(jnp.add, [row[:, k : k + LANES] for k in range(0, width, LANES)])
    sums_ref[0:1] = fold(base_sum)
    sums_ref[1:2] = fold(merged_sum)


def combine(incoming, base, weight):
    vmem = pl.BlockSpec(memory_space=pltpu.VMEM)
    return pl.pallas_call(
        combine_kernel,
        out_shape=[
            jax.ShapeDtypeStruct(base.shape, jnp.float32),
            jax.ShapeDtypeStruct((2, LANES), jnp.float32),
        ],
        in_specs=[vmem] * 3,
        out_specs=[vmem] * 2,
        compiler_params=KERNEL,
        cost_estimate=cost(3_000_000, 3_000_000),
        name="combine",
    )(incoming, base, weight)


def scale_kernel(merged_ref, sums_ref, out_ref):
    ratio = ratio_of(sums_ref)
    for j in range(merged_ref.shape[0]):
        out_ref[j] = (merged_ref[j] * ratio).astype(out_ref.dtype)


def ratio_of(sums_ref):
    total = jnp.sum(sums_ref[...], axis=0)
    base_sq = jnp.sum(total[0:1], axis=1, keepdims=True)
    merged_sq = jnp.sum(total[1:2], axis=1, keepdims=True)
    return jnp.sqrt((base_sq + EPSILON) / (merged_sq + EPSILON))[None]


def scale(merged, sums):
    vmem = pl.BlockSpec(memory_space=pltpu.VMEM)
    return pl.pallas_call(
        scale_kernel,
        out_shape=jax.ShapeDtypeStruct(merged.shape, jnp.bfloat16),
        in_specs=[vmem] * 2,
        out_specs=vmem,
        compiler_params=KERNEL,
        cost_estimate=cost(1_000_000, 1_000_000),
        name="scale",
    )(merged, sums)


def lay_kernel(parts_ref, out_ref):
    reps, own, groups, rows, width = parts_ref.shape
    for r in range(reps):
        for s in range(groups):
            at = (s * reps + r) * width
            out_ref[:, :, at : at + width] = parts_ref[r, :, s]


def lay(parts):
    reps, own, groups, rows, width = parts.shape
    return pl.pallas_call(
        lay_kernel,
        out_shape=jax.ShapeDtypeStruct((own, rows, groups * reps * width), parts.dtype),
        in_specs=[pl.BlockSpec(memory_space=pltpu.VMEM)],
        out_specs=pl.BlockSpec(memory_space=pltpu.VMEM),
        compiler_params=KERNEL,
        cost_estimate=cost(1_000_000, 2_000_000),
        name="lay",
    )(parts)


def sent_to_all(value, axes):
    copies = jnp.broadcast_to(value, (lax.axis_size(axes), *value.shape))
    return lax.all_to_all(copies, axes, split_axis=0, concat_axis=0, tiled=True)


def weights(sel_index, sel_count, scale_num, owner, own, width):
    entries = jnp.arange(sel_index.shape[1], dtype=jnp.int32)
    mine = (entries[None, :] < sel_count[:, None]) & (sel_index // own == owner)
    local = jnp.arange(own, dtype=jnp.int32)
    hit = jnp.any(mine[None] & ((sel_index % own)[None] == local[:, None, None]), axis=2)
    weight = jnp.where(hit, (scale_num.astype(jnp.float32) / DENOMINATOR)[None], 0.0)
    return jnp.broadcast_to(weight[:, :, None], (*weight.shape, width))


def shards(deltas, base, sel_index, sel_count, scale_num):
    task_dev, _, rows, width = deltas.shape
    n_task, n_shard = lax.axis_size(TASK), lax.axis_size(SHARD)
    owners, own = n_task * n_shard, base.shape[0]
    owner = lax.axis_index(OWNER)
    outgoing = pick(sel_index, sel_count, deltas, owners, own)
    incoming = lax.all_to_all(outgoing, OWNER, split_axis=0, concat_axis=0, tiled=True)
    weight = weights(sel_index, sel_count, scale_num, owner, own, width)
    base = jnp.swapaxes(base, 1, 2)
    incoming = incoming.reshape(n_task, n_shard, task_dev, rows, width)
    merged, sums = combine(incoming, base, weight)
    sums = sent_to_all(sums, SAME_LAYER)
    result = scale(merged, sums)
    return lay(sent_to_all(result, "rep"))


def solution(mesh):
    torus = Mesh(
        mesh.devices.reshape(LAYERS, mesh.shape["task"] // LAYERS, mesh.shape["shard"] // 2, 2, mesh.shape["rep"]),
        ("layer", "half", "shard_0", "shard_1", "rep"),
    )
    placed = (P(TASK, None, None, (*SHARD, "rep")), P(OWNER, None, None, "rep"), P(), P(), P())
    return jax.shard_map(shards, mesh=torus, in_specs=placed, out_specs=P(OWNER, None, None), check_vma=False)
```

time: 109 us -> 82.5 us (0.76); the launches traced: 107 us -> 82.2 us
  blocking collectives: 52.1 us -> 33.7 us
  local copies, waits for them, and re-layouts: 10.3 us -> 0.25 us
  Pallas kernels: 0 us -> 6.79 us
  other arithmetic: 4.84 us -> 0.24 us
  waiting for transfers between devices: 25.9 us -> 27.8 us
    psum x4 -> x0, blocking collectives: 36.9 us -> none  [over_axes(): return functools.reduce(lax.psum, axes, shard)]
    all_to_all x1 -> x2, blocking collectives: 15.3 us -> 33.7 us  [sent_to_all(): return lax.all_to_all(copies, axes, split_axis=0, concat_axis=0, tiled=True)]
    pallas_call x0 -> x4, Pallas kernels: none -> 6.79 us  [the longest x1 4.4 us: pick(): pl.pallas_call(functools.partial(pick_kernel, own), out_shape=jax.ShapeDt...]
    gather x7 -> x0, local copies, waits for them, and re-layouts: 5.52 us -> none  [the longest x1 3.09 us: shards(): outgoing = deltas[holder, chosen]]
    select_n x4 -> x2, other arithmetic: 2.15 us -> 0.01 us  [the longest x1 0.01 us: weights(): sel_index % own]
    all_to_all x1, waiting for transfers between devices: 25.9 us -> 27.8 us  [shards(): lax.all_to_all(outgoing, OWNER, split_axis=0, concat_axis=0, tiled=True)]
    another operation x1 -> x0, local copies, waits for them, and re-layouts: 1.59 us -> none  [shards(): return copies.reshape(own_blocks, rows, -1)]
    transpose x1 -> x0, local copies, waits for them, and re-layouts: 1.35 us -> none  [joined_along(): blocks = jnp.moveaxis(blocks, 0, dim)]
  transfers between devices with their start and end apart: 1 -> 1, of which waited for: 1 -> 1; matrix products, arithmetic and copies ran while one was open for 2% -> 0% of each run, Pallas kernels for 0% -> 0%
where the time goes in v1:
time: 82.5 us; the launch traced here: 82.2 us
  blocking collectives  33.7 us (41%)
  waiting for transfers between devices  27.8 us (34%)
  starting transfers between devices  13.3 us (16%)
  Pallas kernels  6.79 us (8%)
    all_to_all x2, blocking collectives, sent_to_all(): return lax.all_to_all(copies, axes, split_axis=0, concat_axis=0, tiled=True)  33.7 us
    all_to_all x1, waiting for transfers between devices, shards(): lax.all_to_all(outgoing, OWNER, split_axis=0, concat_axis=0, tiled=True)  27.8 us
    all_to_all x1, starting transfers between devices, shards(): lax.all_to_all(outgoing, OWNER, split_axis=0, concat_axis=0, tiled=True)  13.3 us
    pallas_call x1, Pallas kernels, pick(): pl.pallas_call(functools.partial(pick_kernel, own), out_shape=jax.ShapeDt...  4.4 us
  transfers between devices with their start and end apart: 1, of which 1 were waited for; matrix products, arithmetic and copies ran while one was open for 0% of the time, Pallas kernels for 0%

profile of v1, /device:TPU:1, one launch (start us, length us, event | category | flops | bytes accessed | tf_op | source)
XLA Modules:
  0.0 82.2 jit_solution(14458555449303169714)
XLA Ops:
  0.0 0.0 copy-start.1
  0.0 0.0 copy-start.2
  0.0 0.0 copy-start
  0.0 0.0 copy-start.3
  0.0 4.4 %pick.1 = bf16[64,2,16,256]{3,2,1,0:T(8,128)(2,1)} custom-call(s32[16,64]{1,0:T(8,128)} %sel_ref.1, s32[16]{0:T(128)} %count_ref.1, bf16[2,256,16,256]{3,2,1,0:T(8,128)(2,1)} %deltas_ref.1), custom_call_target="tpu_custom_call" | custom-call | flops 10000000 | bytes 2097152 | tf_op jit(solution)/shard_map/pick/pallas_call | solution.py:62
  4.4 13.3 %all-to-all-start = ((bf16[64,2,16,256]{3,2,1,0:T(8,128)(2,1)}), bf16[64,2,16,256]{3,2,1,0:T(8,128)(2,1)S(1)}, u32[]{:S(2)}, u32[]{:S(2)}) async-start(bf16[64,2,16,256]{3,2,1,0:T(8,128)(2,1)} %pick.1), calls=%async_computation | async-start | bytes 2097152 | tf_op jit(solution)/shard_map/all_to_all | solution.py:182
  17.7 0.0 copy-done
  17.8 0.0 copy-done.1
  17.8 0.0 copy-done.2
  17.8 0.1 fusion.3
  17.9 0.1 fusion.1
  18.0 0.0 copy-done.3
  18.1 27.8 %all-to-all-done = bf16[64,2,16,256]{3,2,1,0:T(8,128)(2,1)S(1)} async-done(((bf16[64,2,16,256]{3,2,1,0:T(8,128)(2,1)}), bf16[64,2,16,256]{3,2,1,0:T(8,128)(2,1)S(1)}, u32[]{:S(2)}, u32[]{:S(2)}) %all-to-all-start) | async-done | bytes 1048608 | tf_op jit(solution)/shard_map/all_to_all | solution.py:182
  45.9 0.1 broadcast_in_dim.32.weight_ref
  45.9 1.0 %combine.1 = (f32[4,8,16,256]{3,2,1,0:T(8,128)S(1)}, f32[2,128]{1,0:T(2,128)S(1)}) custom-call(bf16[8,8,2,16,256]{4,3,2,1,0:T(8,128)(2,1)S(1)} %bitcast.4, bf16[4,8,16,256]{3,2,1,0:T(8,128)(2,1)S(1)} %bitcast.5, f32[4,16,256]{2,1,0:T(8,128)S(1)} %broadcast_in_dim.32.weight_ref), custom_call_target="tpu_custom_call" | custom-call | flops 3000000 | bytes 3000000 | tf_op jit(solution)/shard_map/combine/pallas_call | solution.py:101
  47.0 16.5 %all_to_all.15.sums_ref = f32[64,2,128]{2,1,0:T(2,128)S(1)} all-to-all(f32[64,2,128]{2,1,0:T(2,128)S(1)} %broadcast_in_dim.33), channel_id=1, replica_groups=mesh['layer'=4,'half'=2,'shard_0'=4,'shard_1'=2,'rep'=4] {'half','shard_..., dimensions={0} | all-to-all | bytes 131072 | tf_op jit(solution)/shard_map/all_to_all | solution.py:164
  63.5 0.2 scale.1
  63.8 0.1 broadcast_in_dim.34
  63.9 17.2 %all_to_all.16.parts_ref = bf16[4,4,8,16,256]{4,3,2,1,0:T(8,128)(2,1)S(1)} all-to-all(bf16[4,4,8,16,256]{4,3,2,1,0:T(8,128)(2,1)S(1)} %broadcast_in_dim.34), channel_id=1, replica_groups=mesh['layer'=4,'half'=2,'shard_0'=4,'shard_1'=2,'rep'=4] {'rep'}, dimensions={0} | all-to-all | bytes 2097152 | tf_op jit(solution)/shard_map/all_to_all | solution.py:164
  81.1 1.1 %lay.1 = bf16[4,16,8192]{2,1,0:T(8,128)(2,1)} custom-call(bf16[4,4,8,16,256]{4,3,2,1,0:T(8,128)(2,1)S(1)} %all_to_all.16.parts_ref), custom_call_target="tpu_custom_call" | custom-call | flops 1000000 | bytes 2000000 | tf_op jit(solution)/shard_map/lay/pallas_call | solution.py:151
  (5 shorter events, 0.1 us)
Async XLA Ops:
  0.0 17.8 %copy-start.1 = (s32[16,64]{1,0:T(8,128)S(1)}, s32[16,64]{1,0:T(8,128)}, u32[]{:S(2)}) copy-start(s32[16,64]{1,0:T(8,128)} %sel_ref.1) | copy-start | bytes 12292
  0.0 17.8 %copy-start.2 = (s32[16]{0:T(128)S(1)}, s32[16]{0:T(128)}, u32[]{:S(2)}) copy-start(s32[16]{0:T(128)} %count_ref.1) | copy-start | bytes 196
  0.0 17.7 %copy-start = (bf16[4,16,8,256]{3,2,1,0:T(8,128)(2,1)S(1)}, bf16[4,16,8,256]{3,2,1,0:T(8,128)(2,1)}, u32[]{:S(2)}) copy-start(bf16[4,16,8,256]{3,2,1,0:T(8,128)(2,1)} %param.6) | copy-start | bytes 786436
  0.0 18.0 %copy-start.3 = (s32[16]{0:T(128)S(1)}, s32[16]{0:T(128)}, u32[]{:S(2)}) copy-start(s32[16]{0:T(128)} %param.9) | copy-start | bytes 196
  4.4 41.4 %all-to-all-start = ((bf16[64,2,16,256]{3,2,1,0:T(8,128)(2,1)}), bf16[64,2,16,256]{3,2,1,0:T(8,128)(2,1)S(1)}, u32[]{:S(2)}, u32[]{:S(2)}) async-start(bf16[64,2,16,256]{3,2,1,0:T(8,128)(2,1)} %pick.1), calls=%async_computation | async-start | bytes 2097152 | tf_op jit(solution)/shard_map/all_to_all | solution.py:182
